TPU v7x, 8 devices: a whole 2x2x1 slice. The times are simulated.
8 devices in a mesh: inst: 1 (over z), qy: 2 (over y), qx: 4 (over x, core).
Axes of the slice: x: 2, y: 2, z: 1, core: 2. Of those that a mesh axis runs over, the one named last changes fastest.
Arguments:
- cost_diag: float32 [2097152], P(('inst', 'qx', 'qy'))
- gammas: float32 [2], replicated
- betas: float32 [2], replicated
Outputs:
- output 1: float32 [1], P('inst')
- output 2: float32 [2097152], P(('inst', 'qx', 'qy'))
- output 3: float32 [2097152], P(('inst', 'qx', 'qy'))
All inputs are finite; a program needn't handle non-finite values.
Results may differ from a plain program's by a relative error of at most 0.001.
Values sent between devices are 32-bit elements.
A program may use at most 1 GiB of HBM per device.

v0:
```python
import math
import jax
import jax.numpy as jnp
import numpy as np
from jax import lax
from jax.experimental import pallas as pl
from jax.experimental.pallas import tpu as pltpu
from jax.sharding import PartitionSpec as P

LANES = 128
MESH = pl.DeviceIdType.MESH
HIGHEST = lax.Precision.HIGHEST
ANGLE_MAX = 131072.0
INV_TURN = float(np.float32(1.0 / (2.0 * math.pi)))
TURN_HI = 6.28125
TURN_LO = float(np.float32(2.0 * math.pi - 6.28125))
CHUNKS = 4
DEVICES = 8
PART = 64

SIN_COEFS = [2 * v / 4.0 ** (2 * k + 1) for k, v in enumerate(
    [1.0, -1.6666654611e-1, 8.3321608736e-3, -1.9515295891e-4])]
COS_COEFS = [2 * v / 16.0 ** k for k, v in enumerate(
    [1.0, -0.5, 4.166664568298827e-2, -1.388731625493765e-3, 2.443315711809948e-5])]


def horner(coefs, z):
    acc = coefs[-1] * z + coefs[-2]
    for v in coefs[-3::-1]:
        acc = acc * z + v
    return acc


def double_phase(cost, gamma, scale, quarter=None, offset=None):
    angle = gamma * cost
    turns = angle * INV_TURN
    if quarter is not None:
        turns = turns - quarter
    n = lax.round(turns, lax.RoundingMethod.TO_NEAREST_EVEN)
    r = (n * TURN_HI - angle) + n * TURN_LO
    if offset is not None:
        r = r + offset
    z = r * r
    s = r * horner(SIN_COEFS, z)
    s2 = s * horner(COS_COEFS, z)
    t2 = scale * s2
    return (scale + scale) - t2 * s2, t2 * (2.0 - s * s)


def rotate_pair(x00, x01, x10, x11, cos_full, sin_full):
    u, v = x00 - x11, x00 + x11
    w, y = x01 + x10, x01 - x10
    u, w = cos_full * u - sin_full * w, sin_full * u + cos_full * w
    return v + u, w + y, w - y, v - u


def quot(a, b):
    return a // b if isinstance(a, int) else lax.div(a, jnp.int32(b))


def rest(a, b):
    return a % b if isinstance(a, int) else lax.rem(a, jnp.int32(b))


def popcount_small(k, bits):
    return sum(rest(quot(k, 1 << b), 2) for b in range(bits))


def rotation_power(cos_half, sin_half, bits, scale):
    n = 1 << bits
    row = lax.broadcasted_iota(jnp.int32, (n, n), 0)
    col = lax.broadcasted_iota(jnp.int32, (n, n), 1)
    acc = jnp.full((n, n), scale, jnp.float32)
    for b in range(bits):
        rb, cb = (row >> b) & 1, (col >> b) & 1
        acc = acc * jnp.where(rb == cb, cos_half, jnp.where(rb > cb, sin_half, -sin_half))
    return acc


def row_gates(arr, cos_half, signed, cos_full, sin_full):
    sub = lax.broadcasted_iota(jnp.int32, (8, LANES), 0)
    for b in range(3):
        k = 1 << b
        other = pltpu.roll(arr, k, 1)
        if 2 * k < 8:
            other = jnp.where((sub & k) == 0, pltpu.roll(arr, 8 - k, 1), other)
        arr = cos_half * arr + signed[b] * other
    v = [arr[k] for k in range(32)]
    for q in (1, 4):
        for k in range(32):
            if (k // q) % 4 == 0:
                quad = (k, k + q, k + 2 * q, k + 3 * q)
                for d, value in zip(quad, rotate_pair(*[v[d] for d in quad], cos_full, sin_full)):
                    v[d] = value
    for k in range(16):
        lo, hi = v[k], v[k + 16]
        v[k], v[k + 16] = cos_half * lo - signed[3] * hi, signed[3] * lo + cos_half * hi
    return v


def loop(start, stop, body, carry, steps=1):
    def turn(n, value):
        for k in range(steps):
            value = body(n * steps + k, value)
        return value
    return lax.fori_loop(start // steps, stop // steps, turn, carry)


def half_lanes(h):
    return pl.ds(pl.multiple_of(h * LANES, LANES), LANES)


def run_rows(ref, h, consts, value=None):
    rows = ref.shape[0]
    value = ref[:, half_lanes(h)] if value is None else value
    v = row_gates(value.reshape(rows // 8, 8, LANES), *consts)
    for k in range(rows // 8):
        ref[pl.ds(8 * k, 8), half_lanes(h)] = v[k]


def run_lanes(ref, w):
    if len(ref.shape) == 2:
        halves = [ref.at[pl.ds(k * LANES, LANES)] for k in range(2)]
    else:
        halves = [ref.at[k] for k in range(2)]
    values = [half[...].reshape(-1, ref.shape[-1]) for half in halves]
    values = [jnp.dot(v, w[...], precision=HIGHEST, preferred_element_type=jnp.float32) for v in values]
    for half, v in zip(halves, values):
        half[...] = v.reshape(half.shape)


def cos_sin(v):
    v = jnp.full((8, LANES), v)
    return jnp.cos(v), jnp.sin(v)


def signed_sines(sin_half):
    sub = lax.broadcasted_iota(jnp.int32, (8, LANES), 0)
    return [jnp.where((sub & (1 << b)) == 0, -sin_half, sin_half) for b in range(3)] + [sin_half]


def quarter_tables(tab_a, tab_b):
    low = (lax.broadcasted_iota(jnp.int32, (PART, LANES), 0) * LANES
           + lax.broadcasted_iota(jnp.int32, (PART, LANES), 1))
    pop = popcount(low, 13)
    for k in range(4):
        q = (pop + k) & 3
        tab_a[k] = jnp.where(q == 0, 1.0, jnp.where(q == 2, -1.0, 0.0))
        tab_b[k] = jnp.where(q == 1, 1.0, jnp.where(q == 3, -1.0, 0.0))
    return pop


def gather_kernel(c_hbm, angles, out_re, out_im, out_cost, out_sums,
                  cost, psi, trig, wave, mixed, part, final, w1, w2,
                  tab_q, tab_o, tab_a, tab_b, cmax, ebuf,
                  own_sem, out_sem, keep_sem, sx, sy, srx, sry, sc, rx, ry, rdx, rdy, rc, swave, rwave, se, re_sem, sums_sem):
    qx, qy = lax.axis_index("qx"), lax.axis_index("qy")
    x, core = quot(qx, 2), rest(qx, 2)
    rows = c_hbm.shape[0]
    chunk = rows // CHUNKS
    half = chunk // 2

    def dev(dx, dy, dc):
        return {"qx": lax.rem(x + dx, 2) * 2 + lax.rem(core + dc, 2), "qy": lax.rem(qy + dy, 2)}

    xn, yn, cn = dev(1, 0, 0), dev(0, 1, 0), dev(0, 0, 1)

    own_copy = pltpu.make_async_copy(c_hbm, cost.at[0, 0], own_sem)
    own_copy.start()
    barrier = pltpu.get_barrier_semaphore()
    for neighbour in (xn, yn, cn):
        pl.semaphore_signal(barrier, inc=1, device_id=neighbour, device_id_type=MESH)

    tile = (8, LANES)
    three = (PART // 8, 8, LANES)
    pl.semaphore_wait(barrier, 3)

    def remote(src, dst, ssem, rsem, device):
        return pltpu.make_async_remote_copy(src_ref=src, dst_ref=dst, send_sem=ssem, recv_sem=rsem,
                                            device_id=device, device_id_type=MESH)

    def rows_of(c):
        return pl.ds(c * chunk, chunk)

    def span(c, h):
        return pl.ds(c * chunk + h * half, half)

    def to_x(c):
        return remote(c_hbm.at[rows_of(c)], cost.at[1, 0, rows_of(c)], sx.at[c], rx.at[c], xn)

    def to_y(c):
        return remote(c_hbm.at[rows_of(c)], cost.at[2, 0, rows_of(c)], sy.at[c], ry.at[c], yn)

    def relay_y(c):
        return remote(cost.at[1, 0, span(c, 0)], cost.at[3, 0, span(c, 0)], sry.at[c], rdy.at[c], yn)

    def relay_x(c):
        return remote(cost.at[2, 0, span(c, 1)], cost.at[3, 0, span(c, 1)], srx.at[c], rdx.at[c], xn)

    def to_core(i, c, h):
        src = c_hbm.at[span(c, h)] if i == 0 else cost.at[i, 0, span(c, h)]
        return remote(src, cost.at[i, 1, span(c, h)], sc.at[i, c, h], rc.at[i, c, h], cn)

    def keep(i, k, c):
        return pltpu.make_async_copy(cost.at[i, k, rows_of(c)], out_cost.at[i, k, rows_of(c)], keep_sem.at[i, k, c])

    for c in range(CHUNKS):
        to_x(c).start()
        to_y(c).start()
    for c in range(CHUNKS):
        for h in range(2):
            to_core(0, c, h).start()

    g1, g2, beta1, beta2 = [angles[k] for k in range(4)]
    ch1, sh1 = cos_sin(0.5 * beta1)
    ch2, sh2 = cos_sin(0.5 * beta2)
    cf1, sf1 = cos_sin(beta1)
    cf2, sf2 = cos_sin(beta2)
    pop = quarter_tables(tab_a, tab_b)
    for k in range(4):
        q = ((pop + k) & 3).astype(jnp.float32)
        tab_q[k] = 0.25 * q
        tab_o[k] = q * float(np.float32(0.5 * math.pi))
    signed1, signed2 = signed_sines(sh1), signed_sines(sh2)

    w1[...] = rotation_power(ch1[0:1, 0:1], -sh1[0:1, 0:1], 8, 2.0 ** -6)
    w2[...] = rotation_power(ch2[0:1, 0:1], -sh2[0:1, 0:1], 8, 2.0 ** -3)
    cmax[...] = jnp.zeros(tile, jnp.float32)

    xf, yf, kf = x.astype(jnp.float32), qy.astype(jnp.float32), core.astype(jnp.float32)
    sign_x, sign_y, sign_k = 2.0 * xf - 1.0, 2.0 * yf - 1.0, 2.0 * kf - 1.0
    flip = sign_x * sign_y
    sx1 = -sign_x * sf1
    sx2, sy2 = sign_x * sh2, sign_y * sh2
    contract = [ch2 * ch2, sx2 * ch2, flip * (ch2 * sy2), flip * (sx2 * sy2)]
    spread = [1.0, 1.0, flip, flip]

    consts1 = (ch1, signed1, cf1, sf1)
    consts2 = (ch2, signed2, cf2, sf2)

    def phases(i, c, own=True, other=True):
        base = c % 2 + c // 2 + (x if i % 2 == 0 else 1 - x) + (qy if i < 2 else 1 - qy)
        ca, cb = spread[i] * ch1, spread[i] * sign_k * sh1
        def body(n, carry):
            r = pl.ds(pl.multiple_of(c * chunk + n * PART, PART), PART)
            spot = (pl.ds(pl.multiple_of(rest(n, 4) * PART, PART), PART), half_lanes(quot(n, 4)))
            terms = []
            for flag, side, coef in ((own, 0, ca), (other, 1, cb)):
                if flag:
                    q = lax.rem(base + popcount_small(n, 3) + (core if side == 0 else 1 - core), 4)
                    terms.append(double_phase(cost[i, side, r].reshape(three), g1, coef,
                                              tab_q[q].reshape(three), tab_o[q].reshape(three)))
            if not own:
                terms.append([psi[k, i, c, *spot].reshape(three) for k in range(2)])
            for k in range(2):
                u = terms[0][k] if len(terms) == 1 else terms[0][k] + terms[1][k]
                psi[k, i, c, *spot] = u.reshape(PART, LANES)
            if own:
                v = cost[i, 0, r].reshape(three)
                for k, u in enumerate(double_phase(v, g2, contract[i])):
                    trig[k, i, r] = u.reshape(PART, LANES)
                if i == 0:
                    cmax[...] = jnp.maximum(cmax[...], jnp.abs(v).max(axis=0))
            return carry

        lax.fori_loop(0, chunk // PART, body, 0)

    def rows_loop(i, c):
        def body(n, carry):
            run_rows(psi.at[quot(n, 2), i, c], rest(n, 2), consts1)
            return carry
        lax.fori_loop(0, 4, body, 0)

    def place(p):
        return pl.ds(pl.multiple_of(rest(p, half // 8) * 8, 8), 8), half_lanes(quot(p, half // 8))

    def chunk_bits(p, carry):
        for k in range(2):
            for i in range(3):
                v = rotate_pair(*[psi[k, i, c, *place(p)] for c in range(CHUNKS)], cf1, sf1)
                for c in range(CHUNKS):
                    psi[k, i, c, *place(p)] = v[c]
        return carry

    def arrived(i, c):
        if i == 1 or i == 2:
            (to_x if i == 1 else to_y)(c).wait_recv()
            (relay_y if i == 1 else relay_x)(c).start()
        if i == 3:
            relay_y(c).wait_recv()
            to_core(i, c, 0).start()
            relay_x(c).wait_recv()
            to_core(i, c, 1).start()
        elif i > 0:
            for h in range(2):
                to_core(i, c, h).start()
        keep(i, 0, c).start()

    def other_arrived(i, c):
        for h in range(2):
            to_core(i, c, h).wait_recv()
        keep(i, 1, c).start()

    def unit(i, c):
        other_arrived(i, c)
        phases(i, c)
        rows_loop(i, c)

    own_copy.wait()
    for c in range(CHUNKS):
        arrived(0, c)
        unit(0, c)
        if c % 2 == 1:
            run_lanes(psi.at[:, 0, pl.ds(c - 1, 2)], w1)
    for c in range(CHUNKS):
        for i in (1, 2):
            arrived(i, c)
        for i in (1, 2):
            unit(i, c)
        run_lanes(psi.at[:, pl.ds(1, 2), c], w1)
    arrived(3, 0)
    loop(0, chunk // 8, chunk_bits, 0, 4)
    arrived(3, 1)
    unit(3, 0)
    unit(3, 1)
    arrived(3, 2)
    run_lanes(psi.at[:, 3, pl.ds(0, 2)], w1)
    unit(3, 2)
    arrived(3, 3)
    run_lanes(psi.at[:, 3, 2], w1)
    phases(3, 3, other=False)
    other_arrived(3, 3)
    phases(3, 3, own=False)
    rows_loop(3, 3)
    run_lanes(psi.at[:, 3, 3], w1)

    def tail(p, carry):
        r = [pl.ds(pl.multiple_of(c * chunk + p * 8, 8), 8) for c in range(CHUNKS)]
        diag = [rotate_pair(*[psi[k, 3, c, *place(p)] for c in range(CHUNKS)], cf1, sf1) for k in range(2)]
        z = [[], []]
        for c in range(CHUNKS):
            v = [rotate_pair(*[psi[k, i, c, *place(p)] for i in (0, 2, 1)], diag[k][c], cf1, sx1) for k in range(2)]
            sums = None
            for n, i in enumerate((0, 2, 1, 3)):
                (re, im), (tr, ti) = (v[0][n], v[1][n]), (trig[0, i, r[c]], trig[1, i, r[c]])
                term = (re * tr - im * ti, re * ti + im * tr)
                sums = term if sums is None else (sums[0] + term[0], sums[1] + term[1])
            z[0].append(sums[0])
            z[1].append(sums[1])
        for k in range(2):
            for c, value in enumerate(rotate_pair(*z[k], cf2, sf2)):
                wave[quot(p, half // 8), k, c, place(p)[0]] = value
        return carry

    def swap(n):
        spot = (n // 2, slice(None), slice(None), pl.ds(n % 2 * LANES, LANES))
        return remote(wave.at[*spot], part.at[*spot], swave.at[n], rwave.at[n], cn)

    quarter = chunk // 8 // 4
    for n in range(4):
        loop(n * quarter, (n + 1) * quarter, tail, 0, 2)
        swap(n).start()

    sk2 = sign_k * sh2
    for h in range(2):
        for n in range(2):
            swap(2 * h + n).wait_recv()

        def turn(n, carry, h=h):
            k, c = quot(n, CHUNKS), rest(n, CHUNKS)
            shape = (half // 8, 8, LANES)
            run_rows(mixed.at[k, c], h, consts2, ch2 * wave[h, k, c].reshape(shape) + sk2 * part[h, k, c].reshape(shape))
            return carry

        lax.fori_loop(0, 2 * CHUNKS, turn, 0)

    energy = jnp.zeros(tile, jnp.float32)
    outs = []
    for c in range(CHUNKS):
        if c % 2 == 0:
            run_lanes(mixed.at[:, pl.ds(c, 2)], w2)

        def last(p, acc, c=c):
            r = pl.ds(pl.multiple_of(c * chunk + p * PART, PART), PART)
            spot = (pl.ds(pl.multiple_of(rest(p, 4) * PART, PART), PART), half_lanes(quot(p, 4)))
            vr, vi = [mixed[k, c, *spot] for k in range(2)]
            k = lax.rem(popcount_small(p, 3) + c % 2 + c // 2 + x + qy + core, 4)
            final[0, r] = tab_a[k] * vr + tab_b[k] * vi
            final[1, r] = tab_a[k] * vi - tab_b[k] * vr
            return acc + (cost[0, 0, r] * (vr * vr + vi * vi)).reshape(three).sum(axis=0)

        energy = loop(0, chunk // PART, last, energy, 4)
        for k, out in enumerate((out_re, out_im)):
            cp = pltpu.make_async_copy(final.at[k, rows_of(c)], out.at[rows_of(c)], out_sem.at[k, c])
            cp.start()
            outs.append(cp)

    me = qy * 4 + qx
    ebuf[me, 0], ebuf[me, 1] = energy, cmax[...] * jnp.maximum(jnp.abs(g1), jnp.abs(g2))
    sends = []
    for n in range(1, DEVICES):
        d = dev(n // 4, (n // 2) % 2, n % 2)
        sends.append(remote(ebuf.at[me], ebuf.at[me], se.at[n], re_sem.at[n], d))
    for cp in sends:
        cp.start()
    for c in range(CHUNKS):
        to_x(c).wait_send()
        to_y(c).wait_send()
        relay_x(c).wait_send()
        relay_y(c).wait_send()
        swap(c).wait_send()
        for i in range(4):
            for k in range(2):
                to_core(i, c, k).wait_send()
                keep(i, k, c).wait()
    for cp in outs:
        cp.wait()
    for cp in sends:
        cp.wait()
    for k in range(2):
        ebuf[DEVICES, k], ebuf[DEVICES + 1, k] = jnp.full(tile, (g1, g2)[k]), jnp.full(tile, (beta1, beta2)[k])
    sums = pltpu.make_async_copy(ebuf, out_sums, sums_sem)
    sums.start()
    sums.wait()


def final_kernel(in_re, in_im, in_cost, in_sums, out_re, out_im, out_energy,
                 state, cost, psi, w, tab_a, tab_b, sums, energy, out_sem, cost_sem, small_sem):
    rows = in_re.shape[0]
    chunk = rows // CHUNKS
    parts, spots = rows // PART, chunk // 8
    outs = (out_re, out_im)

    def put(k, c, src):
        r = pl.ds(c * chunk, chunk)
        return pltpu.make_async_copy(src.at[r], outs[k].at[r], out_sem.at[k, c])

    def put_all(srcs):
        return [put(k, c, srcs[k]) for c in range(CHUNKS) for k in range(2)]

    def put_energy(total):
        energy[0] = total * (1.0 / (DEVICES * rows * LANES))
        return pltpu.make_async_copy(energy, out_energy, small_sem.at[1])

    def run(copies):
        for cp in copies:
            cp.start()
        return copies

    def finish(copies):
        for cp in copies:
            cp.wait()

    moves = run(put_all((in_re, in_im)))
    finish(run([pltpu.make_async_copy(in_sums, sums, small_sem.at[0])]))
    total, largest = sums[0, 0], sums[0, 1]
    for n in range(1, DEVICES):
        total, largest = total + sums[n, 0], jnp.maximum(largest, sums[n, 1])
    moves += run([put_energy(jnp.sum(total))])
    small = jnp.max(largest) <= ANGLE_MAX
    finish(moves)

    @pl.when(jnp.logical_not(small))
    def _():
        qx, qy = lax.axis_index("qx"), lax.axis_index("qy")
        fetch = []
        for a in range(DEVICES):
            i = lax.rem(a // 4 + qx // 2, 2) + 2 * lax.rem(a % 2 + qy, 2)
            fetch.append(pltpu.make_async_copy(in_cost.at[i, lax.rem(a // 2 + qx, 2)], cost.at[a], cost_sem.at[a]))
        run(fetch)
        quarter_tables(tab_a, tab_b)
        finish(fetch)

        def part_of(n):
            a, p = quot(n, parts), rest(n, parts)
            c, q = quot(p, chunk // PART), rest(p, chunk // PART)
            spot = (a, c, pl.ds(pl.multiple_of(rest(q, 4) * PART, PART), PART), half_lanes(quot(q, 4)))
            k = lax.rem(popcount_small(p, 5) + popcount_small(a, 3), 4)
            return a, pl.ds(pl.multiple_of(p * PART, PART), PART), spot, k

        def tile_of(p):
            return pl.ds(pl.multiple_of(rest(p, spots // 2) * 8, 8), 8), half_lanes(quot(p, spots // 2))

        for layer in range(2):
            gamma, beta = [jnp.max(sums[DEVICES + k, layer]) for k in range(2)]
            ch, sh = cos_sin(0.5 * beta)
            cf, sf = cos_sin(beta)

            def phase(n, carry):
                a, r, spot, k = part_of(n)
                t = gamma * cost[a, r]
                vr, vi = jnp.cos(t), -jnp.sin(t)
                qr, qi = (tab_a[k], tab_b[k]) if layer == 0 else (psi[0, *spot], psi[1, *spot])
                psi[0, *spot] = vr * qr - vi * qi
                psi[1, *spot] = vr * qi + vi * qr
                return carry

            lax.fori_loop(0, DEVICES * parts, phase, 0)
            w[...] = rotation_power(ch[0:1, 0:1], -sh[0:1, 0:1], 8, 2.0 ** -4)
            consts = (ch, signed_sines(sh), cf, sf)

            def within(n, carry):
                ref = psi.at[rest(n, 2), quot(n, 2 * CHUNKS), rest(quot(n, 2), CHUNKS)]
                for h in range(2):
                    run_rows(ref, h, consts)
                run_lanes(ref, w)
                return carry

            lax.fori_loop(0, 16 * CHUNKS, within, 0)

            def chunk_bits(n, carry):
                a, p = quot(n, spots), rest(n, spots)
                for k in range(2):
                    v = [psi[k, a, c, *tile_of(p)] for c in range(CHUNKS)]
                    for c, value in enumerate(rotate_pair(*v, cf, sf)):
                        psi[k, a, c, *tile_of(p)] = value
                return carry

            lax.fori_loop(0, DEVICES * spots, chunk_bits, 0)

            def top_bits(n, carry):
                c, p = quot(n, spots), rest(n, spots)
                for k in range(2):
                    v = [psi[k, a, c, *tile_of(p)] for a in range(8)]
                    v = rotate_pair(*v[:4], cf, sf) + rotate_pair(*v[4:], cf, sf)
                    for a in range(4):
                        psi[k, a, c, *tile_of(p)] = ch * v[a] - sh * v[a + 4]
                        psi[k, a + 4, c, *tile_of(p)] = sh * v[a] + ch * v[a + 4]
                return carry

            lax.fori_loop(0, CHUNKS * spots, top_bits, 0)

        def add(n, acc):
            a, r, spot, _ = part_of(n)
            vr, vi = psi[0, *spot], psi[1, *spot]
            return acc + (cost[a, r] * (vr * vr + vi * vi)).reshape(PART // 8, 8, LANES).sum(axis=0)

        total = jnp.sum(lax.fori_loop(0, DEVICES * parts, add, jnp.zeros((8, LANES), jnp.float32)))
        def turn(p, carry):
            _, r, spot, k = part_of((qx * 2 + qy) * parts + p)
            vr, vi, ta, tb = psi[0, *spot], psi[1, *spot], tab_a[k], tab_b[k]
            state[0, r] = ta * vr + tb * vi
            state[1, r] = ta * vi - tb * vr
            return carry

        lax.fori_loop(0, parts, turn, 0)
        finish(run(put_all((state.at[0], state.at[1])) + [put_energy(total)]))


def simulate(cost_rows, gammas, betas):
    rows = cost_rows.shape[0]
    f32 = jnp.float32
    state = jax.ShapeDtypeStruct((rows, LANES), f32)
    near = pl.BlockSpec(memory_space=pl.ANY)
    dma = pltpu.SemaphoreType.DMA
    full = pltpu.VMEM((2, rows, LANES), f32)
    blocks = pltpu.VMEM((2, 4, rows, LANES), f32)
    table = pltpu.VMEM((4, PART, LANES), f32)
    four = dma((CHUNKS,))
    tiles = pltpu.VMEM((DEVICES + 2, 2, 8, LANES), f32)
    halves = pltpu.VMEM((2, 2, CHUNKS, 2 * LANES, LANES), f32)

    def square(*lead):
        return pltpu.VMEM(lead + (2 * LANES, 2 * LANES), f32)

    s_re, s_im, costs, sums = pl.pallas_call(
        gather_kernel,
        out_shape=(state, state, jax.ShapeDtypeStruct((4, 2, rows, LANES), f32),
                   jax.ShapeDtypeStruct((DEVICES + 2, 2, 8, LANES), f32)),
        in_specs=[near, pl.BlockSpec(memory_space=pltpu.SMEM)],
        out_specs=(near,) * 4,
        scratch_shapes=[
            pltpu.VMEM((4, 2, rows, LANES), f32), square(2, 4, CHUNKS), blocks,
            halves, square(2, CHUNKS), halves, full, square(), square(),
            table, table, table, table, pltpu.VMEM((8, LANES), f32), tiles,
            dma, dma((2, 4)), dma((4, 2, 4)), four, four, four, four, dma((4, 4, 2)),
            four, four, four, four, dma((4, 4, 2)), four, four, dma((DEVICES,)), dma((DEVICES,)), dma],
        compiler_params=pltpu.CompilerParams(collective_id=0, has_side_effects=True,
                                             vmem_limit_bytes=52736 << 10),
    )(cost_rows, jnp.concatenate([gammas, betas]))
    return pl.pallas_call(
        final_kernel,
        out_shape=(state, state, jax.ShapeDtypeStruct((1,), f32)),
        in_specs=[near] * 4,
        out_specs=(near,) * 3,
        scratch_shapes=[
            full, pltpu.VMEM((8, rows, LANES), f32), square(2, 8, CHUNKS), square(), table, table,
            tiles, pltpu.SMEM((1,), f32), dma((2, 4)), dma((DEVICES,)), dma((2,))],
        compiler_params=pltpu.CompilerParams(vmem_limit_bytes=52224 << 10),
    )(s_re, s_im, costs, sums)


def popcount(values, bits):
    return sum((values >> b) & 1 for b in range(bits))


def solution(mesh):
    state_spec = P(('inst', 'qx', 'qy'))

    def device_body(cost_local, gammas, betas):
        local_len = cost_local.shape[0]
        s_re, s_im, energy = simulate(cost_local.reshape(local_len // LANES, LANES), gammas, betas)
        return energy, s_re.reshape(local_len), s_im.reshape(local_len)

    return jax.shard_map(device_body, mesh=mesh, in_specs=(state_spec, P(), P()),
                         out_specs=(P('inst'), state_spec, state_spec), check_vma=False)
```

profile of v0, /device:TPU:0, one launch (start us, length us, event | category | flops | bytes accessed | tf_op | source)
XLA Modules:
  0.0 61.2 jit_solution(9990811557391139802)
XLA Ops:
  0.6 0.7 %pad_maximum_fusion.angles = f32[4]{0:T(128)S(1)} fusion(f32[2]{0:T(128)} %param.5, f32[2]{0:T(128)} %param.4), kind=kLoop, calls=%fused_computation | loop fusion | flops 4 | bytes 32 | tf_op jit(solution)/shard_map/concatenate | solution.py:580
  1.4 58.2 %shard_map.58 = (f32[2048,128]{1,0:T(8,128)S(1)}, f32[2048,128]{1,0:T(8,128)S(1)}, f32[4,2,2048,128]{3,2,1,0:T(8,128)}, f32[10,2,8,128]{3,2,1,0:T(8,128)S(1)}) custom-call(f32[2048,128]{1,0:T(8,128)} %bitcast.3, f32[4]{0:T(128)S(1)} %pad_maximum_fusion.angles), custom_call_target="tpu_custom_call" | custom-call | tf_op jit(solution)/shard_map/pallas_call | solution.py:566
  59.6 1.5 %shard_map.59 = (f32[2048,128]{1,0:T(8,128)}, f32[2048,128]{1,0:T(8,128)}, f32[1]{0:T(128)}) custom-call(f32[2048,128]{1,0:T(8,128)S(1)} %get-tuple-element.10.in_re, f32[2048,128]{1,0:T(8,128)S(1)} %get-tuple-element.11.in_im, f32[4,2,2048,128]{3,2,1,0:T(8,128)} %get-tuple-element.12.in_cost, f32[10,2,8,128]{3,2,1,0:T(8,128)S(1)} %get-tuple-element.13.in_sums), custom_call_target="tpu_custom_call" | custom-call | tf_op jit(solution)/shard_map/pallas_call | solution.py:581
where the time goes:
time: 61.3 us; the launch traced here: 61.2 us
  Pallas kernels  59.7 us (97%)
  between operations  0.8 us (1%)
  other arithmetic  0.75 us (1%)
    pallas_call x1, Pallas kernels, simulate(): pl.pallas_call(gather_kernel, out_shape=(state, state, jax.ShapeDtypeStru...  58.2 us
    pallas_call x1, Pallas kernels, simulate(): pl.pallas_call(final_kernel, out_shape=(state, state, jax.ShapeDtypeStruc...  1.48 us

commit v1 on v0

--- a/solution.py
+++ b/solution.py
@@ -15,6 +15,7 @@
 TURN_HI = 6.28125
 TURN_LO = float(np.float32(2.0 * math.pi - 6.28125))
 CHUNKS = 4
+BOTH = range(2)
 DEVICES = 8
 PART = 64
 
@@ -78,13 +79,9 @@
 
 
 def row_gates(arr, cos_half, signed, cos_full, sin_full):
-    sub = lax.broadcasted_iota(jnp.int32, (8, LANES), 0)
+    sub = lax.broadcasted_iota(jnp.int32, arr.shape, 1)
     for b in range(3):
-        k = 1 << b
-        other = pltpu.roll(arr, k, 1)
-        if 2 * k < 8:
-            other = jnp.where((sub & k) == 0, pltpu.roll(arr, 8 - k, 1), other)
-        arr = cos_half * arr + signed[b] * other
+        arr = cos_half * arr + signed[b] * jnp.take_along_axis(arr, sub ^ (1 << b), axis=1)
     v = [arr[k] for k in range(32)]
     for q in (1, 4):
         for k in range(32):
@@ -120,9 +117,9 @@
 
 def run_lanes(ref, w):
     if len(ref.shape) == 2:
-        halves = [ref.at[pl.ds(k * LANES, LANES)] for k in range(2)]
+        halves = [ref.at[pl.ds(k * LANES, LANES)] for k in BOTH]
     else:
-        halves = [ref.at[k] for k in range(2)]
+        halves = [ref.at[k] for k in BOTH]
     values = [half[...].reshape(-1, ref.shape[-1]) for half in halves]
     values = [jnp.dot(v, w[...], precision=HIGHEST, preferred_element_type=jnp.float32) for v in values]
     for half, v in zip(halves, values):
@@ -152,7 +149,7 @@
 
 def gather_kernel(c_hbm, angles, out_re, out_im, out_cost, out_sums,
                   cost, psi, trig, wave, mixed, part, final, w1, w2,
-                  tab_q, tab_o, tab_a, tab_b, cmax, ebuf,
+                  tab_q, tab_o, tab_a, tab_b, cmax, mine,
                   own_sem, out_sem, keep_sem, sx, sy, srx, sry, sc, rx, ry, rdx, rdy, rc, swave, rwave, se, re_sem, sums_sem):
     qx, qy = lax.axis_index("qx"), lax.axis_index("qy")
     x, core = quot(qx, 2), rest(qx, 2)
@@ -165,8 +162,10 @@
 
     xn, yn, cn = dev(1, 0, 0), dev(0, 1, 0), dev(0, 0, 1)
 
-    own_copy = pltpu.make_async_copy(c_hbm, cost.at[0, 0], own_sem)
-    own_copy.start()
+    own_copies = [pltpu.make_async_copy(c_hbm.at[pl.ds(c * chunk, chunk)], cost.at[0, 0, pl.ds(c * chunk, chunk)],
+                                        own_sem.at[c]) for c in range(CHUNKS)]
+    for cp in own_copies:
+        cp.start()
     barrier = pltpu.get_barrier_semaphore()
     for neighbour in (xn, yn, cn):
         pl.semaphore_signal(barrier, inc=1, device_id=neighbour, device_id_type=MESH)
@@ -198,8 +197,7 @@
         return remote(cost.at[2, 0, span(c, 1)], cost.at[3, 0, span(c, 1)], srx.at[c], rdx.at[c], xn)
 
     def to_core(i, c, h):
-        src = c_hbm.at[span(c, h)] if i == 0 else cost.at[i, 0, span(c, h)]
-        return remote(src, cost.at[i, 1, span(c, h)], sc.at[i, c, h], rc.at[i, c, h], cn)
+        return remote(cost.at[i, 0, span(c, h)], cost.at[i, 1, span(c, h)], sc.at[i, c, h], rc.at[i, c, h], cn)
 
     def keep(i, k, c):
         return pltpu.make_async_copy(cost.at[i, k, rows_of(c)], out_cost.at[i, k, rows_of(c)], keep_sem.at[i, k, c])
@@ -208,10 +206,15 @@
         to_x(c).start()
         to_y(c).start()
     for c in range(CHUNKS):
-        for h in range(2):
+        own_copies[c].wait()
+        for h in BOTH:
             to_core(0, c, h).start()
 
     g1, g2, beta1, beta2 = [angles[k] for k in range(4)]
+    for k, v in enumerate(((g1, g2), (beta1, beta2))):
+        mine[k + 1] = jnp.concatenate([jnp.full((1, LANES), u) for u in v], axis=0)
+    keep_angles = pltpu.make_async_copy(mine.at[pl.ds(1, 2)], out_sums.at[pl.ds(DEVICES, 2)], sums_sem.at[1])
+    keep_angles.start()
     ch1, sh1 = cos_sin(0.5 * beta1)
     ch2, sh2 = cos_sin(0.5 * beta2)
     cf1, sf1 = cos_sin(beta1)
@@ -251,8 +254,8 @@
                     terms.append(double_phase(cost[i, side, r].reshape(three), g1, coef,
                                               tab_q[q].reshape(three), tab_o[q].reshape(three)))
             if not own:
-                terms.append([psi[k, i, c, *spot].reshape(three) for k in range(2)])
-            for k in range(2):
+                terms.append([psi[k, i, c, *spot].reshape(three) for k in BOTH])
+            for k in BOTH:
                 u = terms[0][k] if len(terms) == 1 else terms[0][k] + terms[1][k]
                 psi[k, i, c, *spot] = u.reshape(PART, LANES)
             if own:
@@ -263,7 +266,7 @@
                     cmax[...] = jnp.maximum(cmax[...], jnp.abs(v).max(axis=0))
             return carry
 
-        lax.fori_loop(0, chunk // PART, body, 0)
+        loop(0, chunk // PART, body, 0, 2)
 
     def rows_loop(i, c):
         def body(n, carry):
@@ -275,7 +278,7 @@
         return pl.ds(pl.multiple_of(rest(p, half // 8) * 8, 8), 8), half_lanes(quot(p, half // 8))
 
     def chunk_bits(p, carry):
-        for k in range(2):
+        for k in BOTH:
             for i in range(3):
                 v = rotate_pair(*[psi[k, i, c, *place(p)] for c in range(CHUNKS)], cf1, sf1)
                 for c in range(CHUNKS):
@@ -292,12 +295,12 @@
             relay_x(c).wait_recv()
             to_core(i, c, 1).start()
         elif i > 0:
-            for h in range(2):
+            for h in BOTH:
                 to_core(i, c, h).start()
         keep(i, 0, c).start()
 
     def other_arrived(i, c):
-        for h in range(2):
+        for h in BOTH:
             to_core(i, c, h).wait_recv()
         keep(i, 1, c).start()
 
@@ -306,7 +309,6 @@
         phases(i, c)
         rows_loop(i, c)
 
-    own_copy.wait()
     for c in range(CHUNKS):
         arrived(0, c)
         unit(0, c)
@@ -336,10 +338,10 @@
 
     def tail(p, carry):
         r = [pl.ds(pl.multiple_of(c * chunk + p * 8, 8), 8) for c in range(CHUNKS)]
-        diag = [rotate_pair(*[psi[k, 3, c, *place(p)] for c in range(CHUNKS)], cf1, sf1) for k in range(2)]
+        diag = [rotate_pair(*[psi[k, 3, c, *place(p)] for c in range(CHUNKS)], cf1, sf1) for k in BOTH]
         z = [[], []]
         for c in range(CHUNKS):
-            v = [rotate_pair(*[psi[k, i, c, *place(p)] for i in (0, 2, 1)], diag[k][c], cf1, sx1) for k in range(2)]
+            v = [rotate_pair(*[psi[k, i, c, *place(p)] for i in (0, 2, 1)], diag[k][c], cf1, sx1) for k in BOTH]
             sums = None
             for n, i in enumerate((0, 2, 1, 3)):
                 (re, im), (tr, ti) = (v[0][n], v[1][n]), (trig[0, i, r[c]], trig[1, i, r[c]])
@@ -347,24 +349,24 @@
                 sums = term if sums is None else (sums[0] + term[0], sums[1] + term[1])
             z[0].append(sums[0])
             z[1].append(sums[1])
-        for k in range(2):
+        for k in BOTH:
             for c, value in enumerate(rotate_pair(*z[k], cf2, sf2)):
                 wave[quot(p, half // 8), k, c, place(p)[0]] = value
         return carry
 
     def swap(n):
-        spot = (n // 2, slice(None), slice(None), pl.ds(n % 2 * LANES, LANES))
+        spot = (n // 4, slice(None), slice(None), pl.ds(n % 4 * PART, PART))
         return remote(wave.at[*spot], part.at[*spot], swave.at[n], rwave.at[n], cn)
 
-    quarter = chunk // 8 // 4
-    for n in range(4):
-        loop(n * quarter, (n + 1) * quarter, tail, 0, 2)
+    piece = PART // 8
+    for n in range(DEVICES):
+        loop(n * piece, (n + 1) * piece, tail, 0, 2)
         swap(n).start()
 
     sk2 = sign_k * sh2
-    for h in range(2):
-        for n in range(2):
-            swap(2 * h + n).wait_recv()
+    for h in BOTH:
+        for n in range(4):
+            swap(4 * h + n).wait_recv()
 
         def turn(n, carry, h=h):
             k, c = quot(n, CHUNKS), rest(n, CHUNKS)
@@ -383,7 +385,7 @@
         def last(p, acc, c=c):
             r = pl.ds(pl.multiple_of(c * chunk + p * PART, PART), PART)
             spot = (pl.ds(pl.multiple_of(rest(p, 4) * PART, PART), PART), half_lanes(quot(p, 4)))
-            vr, vi = [mixed[k, c, *spot] for k in range(2)]
+            vr, vi = [mixed[k, c, *spot] for k in BOTH]
             k = lax.rem(popcount_small(p, 3) + c % 2 + c // 2 + x + qy + core, 4)
             final[0, r] = tab_a[k] * vr + tab_b[k] * vi
             final[1, r] = tab_a[k] * vi - tab_b[k] * vr
@@ -396,32 +398,30 @@
             outs.append(cp)
 
     me = qy * 4 + qx
-    ebuf[me, 0], ebuf[me, 1] = energy, cmax[...] * jnp.maximum(jnp.abs(g1), jnp.abs(g2))
-    sends = []
-    for n in range(1, DEVICES):
-        d = dev(n // 4, (n // 2) % 2, n % 2)
-        sends.append(remote(ebuf.at[me], ebuf.at[me], se.at[n], re_sem.at[n], d))
+    largest = cmax[...].max(axis=0, keepdims=True) * jnp.maximum(jnp.abs(g1), jnp.abs(g2))
+    mine[0] = jnp.concatenate([energy.sum(axis=0, keepdims=True), largest], axis=0)
+    sends = [remote(mine.at[0], out_sums.at[me], se.at[n], re_sem.at[n], dev(n // 4, (n // 2) % 2, n % 2))
+             for n in range(1, DEVICES)]
     for cp in sends:
         cp.start()
+    keep_mine = pltpu.make_async_copy(mine.at[0], out_sums.at[me], sums_sem.at[0])
+    keep_mine.start()
+    outs += [keep_mine, keep_angles]
     for c in range(CHUNKS):
         to_x(c).wait_send()
         to_y(c).wait_send()
         relay_x(c).wait_send()
         relay_y(c).wait_send()
         swap(c).wait_send()
+        swap(c + CHUNKS).wait_send()
         for i in range(4):
-            for k in range(2):
+            for k in BOTH:
                 to_core(i, c, k).wait_send()
                 keep(i, k, c).wait()
     for cp in outs:
         cp.wait()
     for cp in sends:
         cp.wait()
-    for k in range(2):
-        ebuf[DEVICES, k], ebuf[DEVICES + 1, k] = jnp.full(tile, (g1, g2)[k]), jnp.full(tile, (beta1, beta2)[k])
-    sums = pltpu.make_async_copy(ebuf, out_sums, sums_sem)
-    sums.start()
-    sums.wait()
 
 
 def final_kernel(in_re, in_im, in_cost, in_sums, out_re, out_im, out_energy,
@@ -436,7 +436,7 @@
         return pltpu.make_async_copy(src.at[r], outs[k].at[r], out_sem.at[k, c])
 
     def put_all(srcs):
-        return [put(k, c, srcs[k]) for c in range(CHUNKS) for k in range(2)]
+        return [put(k, c, srcs[k]) for c in range(CHUNKS) for k in BOTH]
 
     def put_energy(total):
         energy[0] = total * (1.0 / (DEVICES * rows * LANES))
@@ -453,11 +453,10 @@
 
     moves = run(put_all((in_re, in_im)))
     finish(run([pltpu.make_async_copy(in_sums, sums, small_sem.at[0])]))
-    total, largest = sums[0, 0], sums[0, 1]
-    for n in range(1, DEVICES):
-        total, largest = total + sums[n, 0], jnp.maximum(largest, sums[n, 1])
+    both = [sums[n] for n in range(DEVICES)]
+    total = sum(v[:1] for v in both[1:]) + both[0][:1]
     moves += run([put_energy(jnp.sum(total))])
-    small = jnp.max(largest) <= ANGLE_MAX
+    small = jnp.max(jnp.stack(both)[:, 1:]) <= ANGLE_MAX
     finish(moves)
 
     @pl.when(jnp.logical_not(small))
@@ -481,8 +480,8 @@
         def tile_of(p):
             return pl.ds(pl.multiple_of(rest(p, spots // 2) * 8, 8), 8), half_lanes(quot(p, spots // 2))
 
-        for layer in range(2):
-            gamma, beta = [jnp.max(sums[DEVICES + k, layer]) for k in range(2)]
+        for layer in BOTH:
+            gamma, beta = [jnp.max(sums[DEVICES + k][layer:layer + 1]) for k in BOTH]
             ch, sh = cos_sin(0.5 * beta)
             cf, sf = cos_sin(beta)
 
@@ -501,7 +500,7 @@
 
             def within(n, carry):
                 ref = psi.at[rest(n, 2), quot(n, 2 * CHUNKS), rest(quot(n, 2), CHUNKS)]
-                for h in range(2):
+                for h in BOTH:
                     run_rows(ref, h, consts)
                 run_lanes(ref, w)
                 return carry
@@ -510,7 +509,7 @@
 
             def chunk_bits(n, carry):
                 a, p = quot(n, spots), rest(n, spots)
-                for k in range(2):
+                for k in BOTH:
                     v = [psi[k, a, c, *tile_of(p)] for c in range(CHUNKS)]
                     for c, value in enumerate(rotate_pair(*v, cf, sf)):
                         psi[k, a, c, *tile_of(p)] = value
@@ -520,7 +519,7 @@
 
             def top_bits(n, carry):
                 c, p = quot(n, spots), rest(n, spots)
-                for k in range(2):
+                for k in BOTH:
                     v = [psi[k, a, c, *tile_of(p)] for a in range(8)]
                     v = rotate_pair(*v[:4], cf, sf) + rotate_pair(*v[4:], cf, sf)
                     for a in range(4):
@@ -556,8 +555,8 @@
     full = pltpu.VMEM((2, rows, LANES), f32)
     blocks = pltpu.VMEM((2, 4, rows, LANES), f32)
     table = pltpu.VMEM((4, PART, LANES), f32)
-    four = dma((CHUNKS,))
-    tiles = pltpu.VMEM((DEVICES + 2, 2, 8, LANES), f32)
+    four, eight = dma((CHUNKS,)), dma((DEVICES,))
+    tiles = pltpu.VMEM((DEVICES + 2, 2, LANES), f32)
     halves = pltpu.VMEM((2, 2, CHUNKS, 2 * LANES, LANES), f32)
 
     def square(*lead):
@@ -566,15 +565,15 @@
     s_re, s_im, costs, sums = pl.pallas_call(
         gather_kernel,
         out_shape=(state, state, jax.ShapeDtypeStruct((4, 2, rows, LANES), f32),
-                   jax.ShapeDtypeStruct((DEVICES + 2, 2, 8, LANES), f32)),
+                   jax.ShapeDtypeStruct((DEVICES + 2, 2, LANES), f32)),
         in_specs=[near, pl.BlockSpec(memory_space=pltpu.SMEM)],
         out_specs=(near,) * 4,
         scratch_shapes=[
             pltpu.VMEM((4, 2, rows, LANES), f32), square(2, 4, CHUNKS), blocks,
             halves, square(2, CHUNKS), halves, full, square(), square(),
-            table, table, table, table, pltpu.VMEM((8, LANES), f32), tiles,
-            dma, dma((2, 4)), dma((4, 2, 4)), four, four, four, four, dma((4, 4, 2)),
-            four, four, four, four, dma((4, 4, 2)), four, four, dma((DEVICES,)), dma((DEVICES,)), dma],
+            table, table, table, table, pltpu.VMEM((8, LANES), f32), pltpu.VMEM((3, 2, LANES), f32),
+            four, dma((2, 4)), dma((4, 2, 4)), four, four, four, four, dma((4, 4, 2)),
+            four, four, four, four, dma((4, 4, 2)), eight, eight, eight, eight, dma((2,))],
         compiler_params=pltpu.CompilerParams(collective_id=0, has_side_effects=True,
                                              vmem_limit_bytes=52736 << 10),
     )(cost_rows, jnp.concatenate([gammas, betas]))

time: 61.3 us -> 59.6 us (0.972)
  Pallas kernels: 59.7 us -> 58 us
    pallas_call x1, Pallas kernels: 58.2 us -> 56.5 us  [simulate(): pl.pallas_call(gather_kernel, out_shape=(state, state, jax.ShapeDtypeStru...]
where the time goes in v1:
time: 59.6 us; the launch traced here: 59.5 us
  Pallas kernels  58 us (97%)
  between operations  0.8 us (1%)
  other arithmetic  0.75 us (1%)
    pallas_call x1, Pallas kernels, simulate(): pl.pallas_call(gather_kernel, out_shape=(state, state, jax.ShapeDtypeStru...  56.5 us
    pallas_call x1, Pallas kernels, simulate(): pl.pallas_call(final_kernel, out_shape=(state, state, jax.ShapeDtypeStruc...  1.48 us

profile of v1, /device:TPU:0, one launch (start us, length us, event | category | flops | bytes accessed | tf_op | source)
XLA Modules:
  0.0 59.5 jit_solution(6317384872301689110)
XLA Ops:
  0.6 0.7 %pad_maximum_fusion.angles = f32[4]{0:T(128)S(1)} fusion(f32[2]{0:T(128)} %param.5, f32[2]{0:T(128)} %param.4), kind=kLoop, calls=%fused_computation | loop fusion | flops 4 | bytes 32 | tf_op jit(solution)/shard_map/concatenate | solution.py:579
  1.4 56.5 %shard_map.58 = (f32[2048,128]{1,0:T(8,128)S(1)}, f32[2048,128]{1,0:T(8,128)S(1)}, f32[4,2,2048,128]{3,2,1,0:T(8,128)}, f32[10,2,128]{2,1,0:T(2,128)S(1)}) custom-call(f32[2048,128]{1,0:T(8,128)} %bitcast.3, f32[4]{0:T(128)S(1)} %pad_maximum_fusion.angles), custom_call_target="tpu_custom_call" | custom-call | tf_op jit(solution)/shard_map/pallas_call | solution.py:565
  57.9 1.5 %shard_map.59 = (f32[2048,128]{1,0:T(8,128)}, f32[2048,128]{1,0:T(8,128)}, f32[1]{0:T(128)}) custom-call(f32[2048,128]{1,0:T(8,128)S(1)} %get-tuple-element.10.in_re, f32[2048,128]{1,0:T(8,128)S(1)} %get-tuple-element.11.in_im, f32[4,2,2048,128]{3,2,1,0:T(8,128)} %get-tuple-element.12.in_cost, f32[10,2,128]{2,1,0:T(2,128)S(1)} %get-tuple-element.13.in_sums), custom_call_target="tpu_custom_call" | custom-call | tf_op jit(solution)/shard_map/pallas_call | solution.py:580

commit v2 on v1

--- a/solution.py
+++ b/solution.py
@@ -147,10 +147,10 @@
     return pop
 
 
-def gather_kernel(c_hbm, angles, out_re, out_im, out_cost, out_sums,
+def gather_kernel(c_hbm, angles_any, out_re, out_im, out_cost, out_sums,
                   cost, psi, trig, wave, mixed, part, final, w1, w2,
-                  tab_q, tab_o, tab_a, tab_b, cmax, mine,
-                  own_sem, out_sem, keep_sem, sx, sy, srx, sry, sc, rx, ry, rdx, rdy, rc, swave, rwave, se, re_sem, sums_sem):
+                  tab_q, tab_o, tab_a, tab_b, cmax, mine, angles,
+                  own_sem, out_sem, keep_sem, sx, sy, srx, sry, sc, rx, ry, rdx, rdy, rc, swave, rwave, se, re_sem, sums_sem, angle_sem):
     qx, qy = lax.axis_index("qx"), lax.axis_index("qy")
     x, core = quot(qx, 2), rest(qx, 2)
     rows = c_hbm.shape[0]
@@ -162,10 +162,10 @@
 
     xn, yn, cn = dev(1, 0, 0), dev(0, 1, 0), dev(0, 0, 1)
 
-    own_copies = [pltpu.make_async_copy(c_hbm.at[pl.ds(c * chunk, chunk)], cost.at[0, 0, pl.ds(c * chunk, chunk)],
-                                        own_sem.at[c]) for c in range(CHUNKS)]
-    for cp in own_copies:
-        cp.start()
+    own_copy = pltpu.make_async_copy(c_hbm, cost.at[0, 0], own_sem)
+    own_copy.start()
+    angle_copy = pltpu.make_async_copy(angles_any, angles, angle_sem)
+    angle_copy.start()
     barrier = pltpu.get_barrier_semaphore()
     for neighbour in (xn, yn, cn):
         pl.semaphore_signal(barrier, inc=1, device_id=neighbour, device_id_type=MESH)
@@ -185,31 +185,31 @@
         return pl.ds(c * chunk + h * half, half)
 
     def to_x(c):
-        return remote(c_hbm.at[rows_of(c)], cost.at[1, 0, rows_of(c)], sx.at[c], rx.at[c], xn)
+        return remote(c_hbm.at[rows_of(c)], cost.at[1, 0, rows_of(c)], sx, rx.at[c], xn)
 
     def to_y(c):
-        return remote(c_hbm.at[rows_of(c)], cost.at[2, 0, rows_of(c)], sy.at[c], ry.at[c], yn)
+        return remote(c_hbm.at[rows_of(c)], cost.at[2, 0, rows_of(c)], sy, ry.at[c], yn)
 
     def relay_y(c):
-        return remote(cost.at[1, 0, span(c, 0)], cost.at[3, 0, span(c, 0)], sry.at[c], rdy.at[c], yn)
+        return remote(cost.at[1, 0, span(c, 0)], cost.at[3, 0, span(c, 0)], sry, rdy.at[c], yn)
 
     def relay_x(c):
-        return remote(cost.at[2, 0, span(c, 1)], cost.at[3, 0, span(c, 1)], srx.at[c], rdx.at[c], xn)
-
-    def to_core(i, c, h):
-        return remote(cost.at[i, 0, span(c, h)], cost.at[i, 1, span(c, h)], sc.at[i, c, h], rc.at[i, c, h], cn)
+        return remote(cost.at[2, 0, span(c, 1)], cost.at[3, 0, span(c, 1)], srx, rdx.at[c], xn)
+
+    def to_core(i, c):
+        return remote(cost.at[i, 0, rows_of(c)], cost.at[i, 1, rows_of(c)], sc, rc.at[i, c], cn)
 
     def keep(i, k, c):
-        return pltpu.make_async_copy(cost.at[i, k, rows_of(c)], out_cost.at[i, k, rows_of(c)], keep_sem.at[i, k, c])
+        return pltpu.make_async_copy(cost.at[i, k, rows_of(c)], out_cost.at[i, k, rows_of(c)], keep_sem)
 
     for c in range(CHUNKS):
         to_x(c).start()
         to_y(c).start()
+    own_copy.wait()
     for c in range(CHUNKS):
-        own_copies[c].wait()
-        for h in BOTH:
-            to_core(0, c, h).start()
-
+        to_core(0, c).start()
+
+    angle_copy.wait()
     g1, g2, beta1, beta2 = [angles[k] for k in range(4)]
     for k, v in enumerate(((g1, g2), (beta1, beta2))):
         mine[k + 1] = jnp.concatenate([jnp.full((1, LANES), u) for u in v], axis=0)
@@ -291,17 +291,13 @@
             (relay_y if i == 1 else relay_x)(c).start()
         if i == 3:
             relay_y(c).wait_recv()
-            to_core(i, c, 0).start()
             relay_x(c).wait_recv()
-            to_core(i, c, 1).start()
-        elif i > 0:
-            for h in BOTH:
-                to_core(i, c, h).start()
+        if i > 0:
+            to_core(i, c).start()
         keep(i, 0, c).start()
 
     def other_arrived(i, c):
-        for h in BOTH:
-            to_core(i, c, h).wait_recv()
+        to_core(i, c).wait_recv()
         keep(i, 1, c).start()
 
     def unit(i, c):
@@ -355,18 +351,19 @@
         return carry
 
     def swap(n):
-        spot = (n // 4, slice(None), slice(None), pl.ds(n % 4 * PART, PART))
-        return remote(wave.at[*spot], part.at[*spot], swave.at[n], rwave.at[n], cn)
-
-    piece = PART // 8
-    for n in range(DEVICES):
-        loop(n * piece, (n + 1) * piece, tail, 0, 2)
+        spot = (quot(n, 4), slice(None), slice(None), pl.ds(pl.multiple_of(rest(n, 4) * PART, PART), PART))
+        return remote(wave.at[*spot], part.at[*spot], swave, rwave.at[quot(n, 4)], cn)
+
+    def piece(n, carry):
+        loop(0, PART // 8, lambda p, v: tail(n * (PART // 8) + p, v), 0, 4)
         swap(n).start()
+        return carry
+
+    lax.fori_loop(0, DEVICES, piece, 0)
 
     sk2 = sign_k * sh2
     for h in BOTH:
-        for n in range(4):
-            swap(4 * h + n).wait_recv()
+        remote(wave.at[h], part.at[h], swave, rwave.at[h], cn).wait_recv()
 
         def turn(n, carry, h=h):
             k, c = quot(n, CHUNKS), rest(n, CHUNKS)
@@ -377,10 +374,9 @@
         lax.fori_loop(0, 2 * CHUNKS, turn, 0)
 
     energy = jnp.zeros(tile, jnp.float32)
-    outs = []
     for c in range(CHUNKS):
-        if c % 2 == 0:
-            run_lanes(mixed.at[:, pl.ds(c, 2)], w2)
+        if c == 0:
+            run_lanes(mixed, w2)
 
         def last(p, acc, c=c):
             r = pl.ds(pl.multiple_of(c * chunk + p * PART, PART), PART)
@@ -393,35 +389,28 @@
 
         energy = loop(0, chunk // PART, last, energy, 4)
         for k, out in enumerate((out_re, out_im)):
-            cp = pltpu.make_async_copy(final.at[k, rows_of(c)], out.at[rows_of(c)], out_sem.at[k, c])
-            cp.start()
-            outs.append(cp)
+            pltpu.make_async_copy(final.at[k, rows_of(c)], out.at[rows_of(c)], out_sem.at[k]).start()
 
     me = qy * 4 + qx
     largest = cmax[...].max(axis=0, keepdims=True) * jnp.maximum(jnp.abs(g1), jnp.abs(g2))
     mine[0] = jnp.concatenate([energy.sum(axis=0, keepdims=True), largest], axis=0)
-    sends = [remote(mine.at[0], out_sums.at[me], se.at[n], re_sem.at[n], dev(n // 4, (n // 2) % 2, n % 2))
+    sends = [remote(mine.at[0], out_sums.at[me], se, re_sem, dev(n // 4, (n // 2) % 2, n % 2))
              for n in range(1, DEVICES)]
     for cp in sends:
         cp.start()
     keep_mine = pltpu.make_async_copy(mine.at[0], out_sums.at[me], sums_sem.at[0])
     keep_mine.start()
-    outs += [keep_mine, keep_angles]
-    for c in range(CHUNKS):
-        to_x(c).wait_send()
-        to_y(c).wait_send()
-        relay_x(c).wait_send()
-        relay_y(c).wait_send()
-        swap(c).wait_send()
-        swap(c + CHUNKS).wait_send()
-        for i in range(4):
-            for k in BOTH:
-                to_core(i, c, k).wait_send()
-                keep(i, k, c).wait()
+    outs = [keep_mine, keep_angles, pltpu.make_async_copy(cost, out_cost, keep_sem)]
+    outs += [pltpu.make_async_copy(final.at[k], out, out_sem.at[k]) for k, out in enumerate((out_re, out_im))]
+    spot, others = pl.ds(0, rows // 2), out_sums.at[pl.ds(0, DEVICES - 1)]
+    for src, dst, sem in ((c_hbm, cost.at[1, 0], sx), (c_hbm, cost.at[2, 0], sy),
+                          (cost.at[1, 0, spot], cost.at[3, 0, spot], sry),
+                          (cost.at[2, 0, spot], cost.at[3, 0, spot], srx),
+                          (cost.at[:, 0], cost.at[:, 1], sc), (wave, part, swave)):
+        remote(src, dst, sem, re_sem, cn).wait_send()
     for cp in outs:
         cp.wait()
-    for cp in sends:
-        cp.wait()
+    remote(others, others, se, re_sem, cn).wait()
 
 
 def final_kernel(in_re, in_im, in_cost, in_sums, out_re, out_im, out_energy,
@@ -431,12 +420,8 @@
     parts, spots = rows // PART, chunk // 8
     outs = (out_re, out_im)
 
-    def put(k, c, src):
-        r = pl.ds(c * chunk, chunk)
-        return pltpu.make_async_copy(src.at[r], outs[k].at[r], out_sem.at[k, c])
-
     def put_all(srcs):
-        return [put(k, c, srcs[k]) for c in range(CHUNKS) for k in BOTH]
+        return [pltpu.make_async_copy(srcs[k], outs[k], out_sem.at[k]) for k in BOTH]
 
     def put_energy(total):
         energy[0] = total * (1.0 / (DEVICES * rows * LANES))
@@ -555,7 +540,7 @@
     full = pltpu.VMEM((2, rows, LANES), f32)
     blocks = pltpu.VMEM((2, 4, rows, LANES), f32)
     table = pltpu.VMEM((4, PART, LANES), f32)
-    four, eight = dma((CHUNKS,)), dma((DEVICES,))
+    two, four = dma((2,)), dma((CHUNKS,))
     tiles = pltpu.VMEM((DEVICES + 2, 2, LANES), f32)
     halves = pltpu.VMEM((2, 2, CHUNKS, 2 * LANES, LANES), f32)
 
@@ -566,14 +551,14 @@
         gather_kernel,
         out_shape=(state, state, jax.ShapeDtypeStruct((4, 2, rows, LANES), f32),
                    jax.ShapeDtypeStruct((DEVICES + 2, 2, LANES), f32)),
-        in_specs=[near, pl.BlockSpec(memory_space=pltpu.SMEM)],
+        in_specs=[near] * 2,
         out_specs=(near,) * 4,
         scratch_shapes=[
             pltpu.VMEM((4, 2, rows, LANES), f32), square(2, 4, CHUNKS), blocks,
             halves, square(2, CHUNKS), halves, full, square(), square(),
-            table, table, table, table, pltpu.VMEM((8, LANES), f32), pltpu.VMEM((3, 2, LANES), f32),
-            four, dma((2, 4)), dma((4, 2, 4)), four, four, four, four, dma((4, 4, 2)),
-            four, four, four, four, dma((4, 4, 2)), eight, eight, eight, eight, dma((2,))],
+            table, table, table, table, pltpu.VMEM((8, LANES), f32), pltpu.VMEM((3, 2, LANES), f32), pltpu.SMEM((4,), f32),
+            dma, two, dma, dma, dma, dma, dma, dma, four, four, four, four, dma((4, CHUNKS)),
+            dma, two, dma, dma, two, dma],
         compiler_params=pltpu.CompilerParams(collective_id=0, has_side_effects=True,
                                              vmem_limit_bytes=52736 << 10),
     )(cost_rows, jnp.concatenate([gammas, betas]))
@@ -584,7 +569,7 @@
         out_specs=(near,) * 3,
         scratch_shapes=[
             full, pltpu.VMEM((8, rows, LANES), f32), square(2, 8, CHUNKS), square(), table, table,
-            tiles, pltpu.SMEM((1,), f32), dma((2, 4)), dma((DEVICES,)), dma((2,))],
+            tiles, pltpu.SMEM((1,), f32), two, dma((DEVICES,)), two],
         compiler_params=pltpu.CompilerParams(vmem_limit_bytes=52224 << 10),
     )(s_re, s_im, costs, sums)
 

time: 59.6 us -> 57.5 us (0.965)
  Pallas kernels: 58 us -> 55.8 us
    pallas_call x1, Pallas kernels: 56.5 us -> 54.4 us  [simulate(): pl.pallas_call(gather_kernel, out_shape=(state, state, jax.ShapeDtypeStru...]
where the time goes in v2:
time: 57.5 us; the launch traced here: 57.4 us
  Pallas kernels  55.8 us (97%)
  between operations  0.8 us (1%)
  other arithmetic  0.75 us (1%)
    pallas_call x1, Pallas kernels, simulate(): pl.pallas_call(gather_kernel, out_shape=(state, state, jax.ShapeDtypeStru...  54.4 us
    pallas_call x1, Pallas kernels, simulate(): pl.pallas_call(final_kernel, out_shape=(state, state, jax.ShapeDtypeStruc...  1.44 us

profile of v2, /device:TPU:0, one launch (start us, length us, event | category | flops | bytes accessed | tf_op | source)
XLA Modules:
  0.0 57.4 jit_solution(16096243704372897165)
XLA Ops:
  0.6 0.7 %pad_maximum_fusion.angles_any = f32[4]{0:T(128)S(1)} fusion(f32[2]{0:T(128)} %param.5, f32[2]{0:T(128)} %param.4), kind=kLoop, calls=%fused_computation | loop fusion | flops 4 | bytes 32 | tf_op jit(solution)/shard_map/concatenate | solution.py:564
  1.4 54.4 %shard_map.58 = (f32[2048,128]{1,0:T(8,128)S(1)}, f32[2048,128]{1,0:T(8,128)S(1)}, f32[4,2,2048,128]{3,2,1,0:T(8,128)}, f32[10,2,128]{2,1,0:T(2,128)S(1)}) custom-call(f32[2048,128]{1,0:T(8,128)} %bitcast.3, f32[4]{0:T(128)S(1)} %pad_maximum_fusion.angles_any), custom_call_target="tpu_custom_call" | custom-call | tf_op jit(solution)/shard_map/pallas_call | solution.py:550
  55.8 1.4 %shard_map.59 = (f32[2048,128]{1,0:T(8,128)}, f32[2048,128]{1,0:T(8,128)}, f32[1]{0:T(128)}) custom-call(f32[2048,128]{1,0:T(8,128)S(1)} %get-tuple-element.10.in_re, f32[2048,128]{1,0:T(8,128)S(1)} %get-tuple-element.11.in_im, f32[4,2,2048,128]{3,2,1,0:T(8,128)} %get-tuple-element.12.in_cost, f32[10,2,128]{2,1,0:T(2,128)S(1)} %get-tuple-element.13.in_sums), custom_call_target="tpu_custom_call" | custom-call | tf_op jit(solution)/shard_map/pallas_call | solution.py:565

commit v3 on v2

--- a/solution.py
+++ b/solution.py
@@ -277,9 +277,9 @@
     def place(p):
         return pl.ds(pl.multiple_of(rest(p, half // 8) * 8, 8), 8), half_lanes(quot(p, half // 8))
 
-    def chunk_bits(p, carry):
+    def chunk_bits(p, carry, blocks=(1, 2)):
         for k in BOTH:
-            for i in range(3):
+            for i in blocks:
                 v = rotate_pair(*[psi[k, i, c, *place(p)] for c in range(CHUNKS)], cf1, sf1)
                 for c in range(CHUNKS):
                     psi[k, i, c, *place(p)] = v[c]
@@ -315,8 +315,11 @@
             arrived(i, c)
         for i in (1, 2):
             unit(i, c)
+        if c == CHUNKS - 1:
+            arrived(3, 0)
         run_lanes(psi.at[:, pl.ds(1, 2), c], w1)
-    arrived(3, 0)
+        if c == 0:
+            loop(0, chunk // 8, lambda p, v: chunk_bits(p, v, (0,)), 0, 4)
     loop(0, chunk // 8, chunk_bits, 0, 4)
     arrived(3, 1)
     unit(3, 0)
@@ -329,7 +332,9 @@
     phases(3, 3, other=False)
     other_arrived(3, 3)
     phases(3, 3, own=False)
-    rows_loop(3, 3)
+    for k in BOTH:
+        for h in BOTH:
+            run_rows(psi.at[k, 3, 3], h, consts1)
     run_lanes(psi.at[:, 3, 3], w1)
 
     def tail(p, carry):

time: 57.5 us -> 57.2 us (level)
  no operation moved by 1% of the time
where the time goes in v3:
time: 57.2 us; the launch traced here: 57.1 us
  Pallas kernels  55.5 us (97%)
  between operations  0.8 us (1%)
  other arithmetic  0.75 us (1%)
    pallas_call x1, Pallas kernels, simulate(): pl.pallas_call(gather_kernel, out_shape=(state, state, jax.ShapeDtypeStru...  54.1 us
    pallas_call x1, Pallas kernels, simulate(): pl.pallas_call(final_kernel, out_shape=(state, state, jax.ShapeDtypeStruc...  1.44 us

profile of v3, /device:TPU:0, one launch (start us, length us, event | category | flops | bytes accessed | tf_op | source)
XLA Modules:
  0.0 57.1 jit_solution(15657995949506695179)
XLA Ops:
  0.6 0.7 %pad_maximum_fusion.angles_any = f32[4]{0:T(128)S(1)} fusion(f32[2]{0:T(128)} %param.5, f32[2]{0:T(128)} %param.4), kind=kLoop, calls=%fused_computation | loop fusion | flops 4 | bytes 32 | tf_op jit(solution)/shard_map/concatenate | solution.py:569
  1.4 54.1 %shard_map.58 = (f32[2048,128]{1,0:T(8,128)S(1)}, f32[2048,128]{1,0:T(8,128)S(1)}, f32[4,2,2048,128]{3,2,1,0:T(8,128)}, f32[10,2,128]{2,1,0:T(2,128)S(1)}) custom-call(f32[2048,128]{1,0:T(8,128)} %bitcast.3, f32[4]{0:T(128)S(1)} %pad_maximum_fusion.angles_any), custom_call_target="tpu_custom_call" | custom-call | tf_op jit(solution)/shard_map/pallas_call | solution.py:555
  55.5 1.4 %shard_map.59 = (f32[2048,128]{1,0:T(8,128)}, f32[2048,128]{1,0:T(8,128)}, f32[1]{0:T(128)}) custom-call(f32[2048,128]{1,0:T(8,128)S(1)} %get-tuple-element.10.in_re, f32[2048,128]{1,0:T(8,128)S(1)} %get-tuple-element.11.in_im, f32[4,2,2048,128]{3,2,1,0:T(8,128)} %get-tuple-element.12.in_cost, f32[10,2,128]{2,1,0:T(2,128)S(1)} %get-tuple-element.13.in_sums), custom_call_target="tpu_custom_call" | custom-call | tf_op jit(solution)/shard_map/pallas_call | solution.py:570

commit v4 on v3

--- a/solution.py
+++ b/solution.py
@@ -356,15 +356,16 @@
         return carry
 
     def swap(n):
-        spot = (quot(n, 4), slice(None), slice(None), pl.ds(pl.multiple_of(rest(n, 4) * PART, PART), PART))
-        return remote(wave.at[*spot], part.at[*spot], swave, rwave.at[quot(n, 4)], cn)
+        spot = (quot(n, 8), slice(None), slice(None), pl.ds(pl.multiple_of(rest(n, 8) * 32, 32), 32))
+        return remote(wave.at[*spot], part.at[*spot], swave, rwave.at[quot(n, 8)], cn)
 
     def piece(n, carry):
-        loop(0, PART // 8, lambda p, v: tail(n * (PART // 8) + p, v), 0, 4)
+        for k in range(4):
+            tail(4 * n + k, carry)
         swap(n).start()
         return carry
 
-    lax.fori_loop(0, DEVICES, piece, 0)
+    lax.fori_loop(0, 2 * DEVICES, piece, 0)
 
     sk2 = sign_k * sh2
     for h in BOTH:
@@ -376,7 +377,7 @@
             run_rows(mixed.at[k, c], h, consts2, ch2 * wave[h, k, c].reshape(shape) + sk2 * part[h, k, c].reshape(shape))
             return carry
 
-        lax.fori_loop(0, 2 * CHUNKS, turn, 0)
+        loop(0, 2 * CHUNKS, turn, 0, 2)
 
     energy = jnp.zeros(tile, jnp.float32)
     for c in range(CHUNKS):

time: 57.2 us -> 57 us (level)
  no operation moved by 1% of the time
where the time goes in v4:
time: 57 us; the launch traced here: 56.9 us
  Pallas kernels  55.3 us (97%)
  between operations  0.8 us (1%)
  other arithmetic  0.75 us (1%)
    pallas_call x1, Pallas kernels, simulate(): pl.pallas_call(gather_kernel, out_shape=(state, state, jax.ShapeDtypeStru...  53.9 us
    pallas_call x1, Pallas kernels, simulate(): pl.pallas_call(final_kernel, out_shape=(state, state, jax.ShapeDtypeStruc...  1.44 us

profile of v4, /device:TPU:0, one launch (start us, length us, event | category | flops | bytes accessed | tf_op | source)
XLA Modules:
  0.0 56.9 jit_solution(3348974224999440982)
XLA Ops:
  0.6 0.7 %pad_maximum_fusion.angles_any = f32[4]{0:T(128)S(1)} fusion(f32[2]{0:T(128)} %param.5, f32[2]{0:T(128)} %param.4), kind=kLoop, calls=%fused_computation | loop fusion | flops 4 | bytes 32 | tf_op jit(solution)/shard_map/concatenate | solution.py:570
  1.4 53.9 %shard_map.58 = (f32[2048,128]{1,0:T(8,128)S(1)}, f32[2048,128]{1,0:T(8,128)S(1)}, f32[4,2,2048,128]{3,2,1,0:T(8,128)}, f32[10,2,128]{2,1,0:T(2,128)S(1)}) custom-call(f32[2048,128]{1,0:T(8,128)} %bitcast.3, f32[4]{0:T(128)S(1)} %pad_maximum_fusion.angles_any), custom_call_target="tpu_custom_call" | custom-call | tf_op jit(solution)/shard_map/pallas_call | solution.py:556
  55.3 1.4 %shard_map.59 = (f32[2048,128]{1,0:T(8,128)}, f32[2048,128]{1,0:T(8,128)}, f32[1]{0:T(128)}) custom-call(f32[2048,128]{1,0:T(8,128)S(1)} %get-tuple-element.10.in_re, f32[2048,128]{1,0:T(8,128)S(1)} %get-tuple-element.11.in_im, f32[4,2,2048,128]{3,2,1,0:T(8,128)} %get-tuple-element.12.in_cost, f32[10,2,128]{2,1,0:T(2,128)S(1)} %get-tuple-element.13.in_sums), custom_call_target="tpu_custom_call" | custom-call | tf_op jit(solution)/shard_map/pallas_call | solution.py:571

commit v5 on v4

--- a/solution.py
+++ b/solution.py
@@ -266,7 +266,7 @@
                     cmax[...] = jnp.maximum(cmax[...], jnp.abs(v).max(axis=0))
             return carry
 
-        loop(0, chunk // PART, body, 0, 2)
+        loop(0, chunk // PART, body, 0, 4)
 
     def rows_loop(i, c):
         def body(n, carry):

time: 57 us -> 57 us (level)
  no operation moved by 1% of the time
where the time goes in v5:
time: 57 us; the launch traced here: 56.9 us
  Pallas kernels  55.3 us (97%)
  between operations  0.8 us (1%)
  other arithmetic  0.75 us (1%)
    pallas_call x1, Pallas kernels, simulate(): pl.pallas_call(gather_kernel, out_shape=(state, state, jax.ShapeDtypeStru...  53.9 us
    pallas_call x1, Pallas kernels, simulate(): pl.pallas_call(final_kernel, out_shape=(state, state, jax.ShapeDtypeStruc...  1.44 us

profile of v5, /device:TPU:0, one launch (start us, length us, event | category | flops | bytes accessed | tf_op | source)
XLA Modules:
  0.0 56.9 jit_solution(11053794836235263629)
XLA Ops:
  0.6 0.7 %pad_maximum_fusion.angles_any = f32[4]{0:T(128)S(1)} fusion(f32[2]{0:T(128)} %param.5, f32[2]{0:T(128)} %param.4), kind=kLoop, calls=%fused_computation | loop fusion | flops 4 | bytes 32 | tf_op jit(solution)/shard_map/concatenate | solution.py:570
  1.4 53.9 %shard_map.58 = (f32[2048,128]{1,0:T(8,128)S(1)}, f32[2048,128]{1,0:T(8,128)S(1)}, f32[4,2,2048,128]{3,2,1,0:T(8,128)}, f32[10,2,128]{2,1,0:T(2,128)S(1)}) custom-call(f32[2048,128]{1,0:T(8,128)} %bitcast.3, f32[4]{0:T(128)S(1)} %pad_maximum_fusion.angles_any), custom_call_target="tpu_custom_call" | custom-call | tf_op jit(solution)/shard_map/pallas_call | solution.py:556
  55.3 1.4 %shard_map.59 = (f32[2048,128]{1,0:T(8,128)}, f32[2048,128]{1,0:T(8,128)}, f32[1]{0:T(128)}) custom-call(f32[2048,128]{1,0:T(8,128)S(1)} %get-tuple-element.10.in_re, f32[2048,128]{1,0:T(8,128)S(1)} %get-tuple-element.11.in_im, f32[4,2,2048,128]{3,2,1,0:T(8,128)} %get-tuple-element.12.in_cost, f32[10,2,128]{2,1,0:T(2,128)S(1)} %get-tuple-element.13.in_sums), custom_call_target="tpu_custom_call" | custom-call | tf_op jit(solution)/shard_map/pallas_call | solution.py:571
